TPU v7x, 32 devices: a whole 2x2x4 slice. The times are simulated.
32 devices in a mesh: groups: 2 (over y), fsdp: 4 (over z), tensor: 4 (over x, core).
Axes of the slice: x: 2, y: 2, z: 4, core: 2. Of those that a mesh axis runs over, the one named last changes fastest.
Arguments:
- tokens: bfloat16 [2048, 4608], P(('groups', 'fsdp'), 'tensor'), parts along dimension 0, may hold values from -100 to 100
- norm_gain: bfloat16 [4608], P('tensor'), may hold values from 0.25 to 1.75
- w_query: bfloat16 [4608, 4096], P('fsdp', 'tensor'), may hold values from -0.5 to 0.5
- w_key: bfloat16 [4608, 2048], P('fsdp', 'tensor'), may hold values from -0.09375 to 0.09375
- w_value: bfloat16 [4608, 2048], P('fsdp', 'tensor'), may hold values from -0.09375 to 0.09375
- w_out: bfloat16 [4096, 4608], P('tensor', 'fsdp'), may hold values from -0.5 to 0.5
- post_gain: bfloat16 [4608], P('tensor'), may hold values from 0.25 to 1.75
Outputs:
- mixed: float32 [2048, 4608], P(('groups', 'fsdp'), 'tensor'), parts along dimension 0
There are 2 independent parts, one for each index of `groups`. A program takes and returns all parts, laid end to end along the dimension named above; an argument that names none is the same for every part. Nothing has to cross between parts.
All inputs are finite; a program needn't handle non-finite values.
Results may differ from a plain program's by a relative error of at most 0.0053.
Values may be sent and summed in bfloat16 or wider, within the bound.
A program may use at most 128 MiB of HBM per device.

v0:
```python
import jax
import jax.numpy as jnp
from jax import lax
from jax.sharding import PartitionSpec as P

HEAD_DIM = 128
eps_norm = 1e-06
soft_cap = 50.0
attn_scale = 144.0 ** (-0.5)
rope_base = 10000.0


def rotate(values, position):
    head_dim = values.shape[-1]
    half = head_dim // 2
    freq = rope_base ** (-(jnp.arange(half, dtype=jnp.float32) * 2.0 / head_dim))
    angle = position.astype(jnp.float32)[:, None] * freq[None, :]
    cosine = jnp.cos(angle)[:, None, :]
    sine = jnp.sin(angle)[:, None, :]
    first = values[..., :half]
    second = values[..., half:]
    return jnp.concatenate(
        [first * cosine - second * sine, second * cosine + first * sine], axis=-1
    )


def attend(query, keys, values, position):
    count, heads, head_dim = query.shape
    kv_count = keys.shape[1]
    grouped = query.reshape(count, kv_count, heads // kv_count, head_dim)
    scores = (
        jnp.einsum("nkgd,mkd->kgnm", grouped, keys, preferred_element_type=jnp.float32) * attn_scale
    )
    capped = soft_cap * jnp.tanh(scores / soft_cap)
    allowed = position[None, :] <= position[:, None]
    weights = jnp.where(allowed, jnp.exp(capped), 0.0)
    probs = (weights / jnp.sum(weights, axis=-1, keepdims=True)).astype(jnp.bfloat16)
    mixed = jnp.einsum("kgnm,mkd->nkgd", probs, values, preferred_element_type=jnp.float32)
    return mixed.reshape(count, heads * head_dim).astype(jnp.bfloat16)


def swap_pairs(n_fsdp, n_tensor, turn):
    ratio = n_fsdp // n_tensor
    pairs = []
    for f in range(n_fsdp):
        for t in range(n_tensor):
            j = (f + turn) % ratio
            pairs.append((f * n_tensor + t, (t * ratio + j) * n_tensor + f // ratio))
    return pairs


def to_rows(block, n_fsdp, n_tensor):
    rows = block.shape[0]
    ratio = n_fsdp // n_tensor
    width = block.shape[1] // ratio
    f = lax.axis_index("fsdp")
    if ratio == 1:
        held = lax.ppermute(block, ("fsdp", "tensor"), swap_pairs(n_fsdp, n_tensor, 0))
    else:
        held = jnp.zeros((ratio, rows, width), block.dtype)
        for turn in range(ratio):
            piece = lax.dynamic_slice_in_dim(block, (f + turn) % ratio * width, width, 1)
            got = lax.ppermute(piece, ("fsdp", "tensor"), swap_pairs(n_fsdp, n_tensor, turn))
            held = lax.dynamic_update_index_in_dim(held, got, (f - turn) % ratio, 0)
        held = held.reshape(ratio * rows, width)
    return lax.all_gather(held, "tensor", axis=0, tiled=True)


def from_rows(summed, rows, n_fsdp, n_tensor):
    ratio = n_fsdp // n_tensor
    width = summed.shape[1]
    f = lax.axis_index("fsdp")
    back = lambda turn: [(b, a) for a, b in swap_pairs(n_fsdp, n_tensor, turn)]
    if ratio == 1:
        return lax.ppermute(summed, ("fsdp", "tensor"), back(0))
    pieces = summed.reshape(ratio, rows, width)
    out = jnp.zeros((rows, ratio * width), summed.dtype)
    for turn in range(ratio):
        piece = lax.dynamic_index_in_dim(pieces, (f - turn) % ratio, 0, keepdims=False)
        got = lax.ppermute(piece, ("fsdp", "tensor"), back(turn))
        out = lax.dynamic_update_slice_in_dim(out, got, (f + turn) % ratio * width, 1)
    return out


def solution(mesh):
    n_fsdp, n_tensor = (mesh.shape["fsdp"], mesh.shape["tensor"])

    def on_device(tokens, norm_gain, w_query, w_key, w_value, w_out, post_gain):
        rows = tokens.shape[0]
        width = tokens.shape[1] * n_tensor
        widened = tokens.astype(jnp.float32)
        total = lax.psum(jnp.sum(widened * widened, axis=1), "tensor")
        normed = (
            widened * lax.rsqrt(total / width + eps_norm)[:, None] * norm_gain.astype(jnp.float32)
        ).astype(jnp.bfloat16)
        mine = to_rows(normed, n_fsdp, n_tensor)
        raw = []
        for piece in (w_query, w_key, w_value):
            part = jnp.dot(mine, piece, preferred_element_type=jnp.float32).astype(jnp.bfloat16)
            parts = lax.all_to_all(part, "fsdp", 0, 0, tiled=True)
            parts = parts.reshape(n_fsdp, rows, piece.shape[1])
            raw.append(jnp.sum(parts.astype(jnp.float32), axis=0))
        query_raw, key_raw, value_raw = raw
        position = jnp.arange(rows, dtype=jnp.int32)
        local_heads = w_query.shape[1] // HEAD_DIM
        local_kv = w_key.shape[1] // HEAD_DIM
        query = rotate(query_raw.reshape(rows, local_heads, HEAD_DIM), position)
        key = rotate(key_raw.reshape(rows, local_kv, HEAD_DIM), position)
        query, key = (query.astype(jnp.bfloat16), key.astype(jnp.bfloat16))
        value = value_raw.astype(jnp.bfloat16).reshape(rows, local_kv, HEAD_DIM)
        attn = attend(query, key, value, position)
        attn_all = lax.all_gather(attn, "fsdp", axis=0, tiled=True)
        part = jnp.dot(attn_all, w_out, preferred_element_type=jnp.float32).astype(jnp.bfloat16)
        summed = lax.psum_scatter(part, "tensor", scatter_dimension=0, tiled=True)
        proj = from_rows(summed, rows, n_fsdp, n_tensor).astype(jnp.float32)
        post_total = lax.psum(jnp.sum(proj * proj, axis=1), "tensor")
        branch = (
            proj * lax.rsqrt(post_total / width + eps_norm)[:, None] * post_gain.astype(jnp.float32)
        )
        return tokens.astype(jnp.float32) + branch

    placed = (
        P(("groups", "fsdp"), "tensor"),
        P("tensor"),
        P("fsdp", "tensor"),
        P("fsdp", "tensor"),
        P("fsdp", "tensor"),
        P("tensor", "fsdp"),
        P("tensor"),
    )
    return jax.shard_map(
        on_device,
        mesh=mesh,
        in_specs=placed,
        out_specs=P(("groups", "fsdp"), "tensor"),
        check_vma=False,
    )
```

profile of v0, /device:TPU:0, one launch (start us, length us, event | category | flops | bytes accessed | tf_op | source)
XLA Modules:
  0.0 329.1 jit_solution(13812048784093894810)
XLA Ops:
  6.5 1.4 fusion.2
  7.9 8.4 %psum.14 = f32[256]{0:T(256)S(1)} all-reduce(f32[256]{0:T(256)S(1)} %fusion.2), channel_id=1, replica_groups=mesh['groups'=2,'fsdp'=4,'tensor'=4] {'tensor'}, use_global_device_ids=true, to_apply=%region_1.0 | all-reduce | flops 256 | bytes 2048 | tf_op jit(solution)/shard_map/psum | solution.py:92
  16.3 0.7 convert_element_type.74
  17.0 1.3 fusion.4
  18.3 0.7 collective-permute-start
  19.0 0.8 copy-done.3
  19.8 0.0 all-gather.3.cloned.1.call-update
  19.9 53.0 %all-gather.3.cloned.1.call-done = bf16[1024,1152]{1,0:T(8,128)(2,1)} async-done(((bf16[256,1152]{1,0:T(8,128)(2,1)}), bf16[1024,1152]{1,0:T(8,128)(2,1)}) %all-gather.3.cloned.1.call-update) | async-done | bytes 2359312 | tf_op jit(solution)/shard_map/all_gather | solution.py:66
  72.9 4.5 %convolution_convert_fusion.2 = bf16[1024,512]{1,0:T(8,128)(2,1)} fusion(bf16[1024,1152]{1,0:T(8,128)(2,1)} %all-gather.3.cloned.1.call-done, bf16[1152,512]{1,0:T(8,128)(2,1)} %param.10), kind=kOutput, calls=%fused_computation.9 | convolution fusion | flops 1208483840 | bytes 4587520 | tf_op jit(solution)/shard_map/dot_general | solution.py:99
  77.3 4.6 %all-to-all-start.1 = ((bf16[4,256,512]{2,1,0:T(8,128)(2,1)}), bf16[4,256,512]{2,1,0:T(8,128)(2,1)S(1)}, u32[]{:S(2)}, u32[]{:S(2)}) async-start(bf16[4,256,512]{2,1,0:T(8,128)(2,1)} %bitcast.36), calls=%async_computation.1 | async-start | bytes 2097152 | tf_op jit(solution)/shard_map/all_to_all | solution.py:100
  81.9 4.5 %convolution_convert_fusion.3 = bf16[1024,512]{1,0:T(8,128)(2,1)} fusion(bf16[1024,1152]{1,0:T(8,128)(2,1)} %all-gather.3.cloned.1.call-done, bf16[1152,512]{1,0:T(8,128)(2,1)} %param.11), kind=kOutput, calls=%fused_computation.10 | convolution fusion | flops 1208483840 | bytes 4587520 | tf_op jit(solution)/shard_map/dot_general | solution.py:99
  86.4 21.6 %all-to-all-done.1 = bf16[4,256,512]{2,1,0:T(8,128)(2,1)S(1)} async-done(((bf16[4,256,512]{2,1,0:T(8,128)(2,1)}), bf16[4,256,512]{2,1,0:T(8,128)(2,1)S(1)}, u32[]{:S(2)}, u32[]{:S(2)}) %all-to-all-start.1) | async-done | bytes 1048608 | tf_op jit(solution)/shard_map/all_to_all | solution.py:100
  108.1 1.0 copy-done.2
  109.0 3.5 %all-to-all-start = ((bf16[4,256,512]{2,1,0:T(8,128)(2,1)}), bf16[4,256,512]{2,1,0:T(8,128)(2,1)S(1)}, u32[]{:S(2)}, u32[]{:S(2)}) async-start(bf16[4,256,512]{2,1,0:T(8,128)(2,1)} %bitcast.35), calls=%async_computation | async-start | bytes 2097152 | tf_op jit(solution)/shard_map/all_to_all | solution.py:100
  112.6 6.6 %convolution_convert_fusion.1 = bf16[1024,1024]{1,0:T(8,128)(2,1)} fusion(bf16[1024,1152]{1,0:T(8,128)(2,1)} %all-gather.3.cloned.1.call-done, bf16[1152,1024]{1,0:T(8,128)(2,1)} %param.9), kind=kOutput, calls=%fused_computation.5 | convolution fusion | flops 2416967680 | bytes 6815744 | tf_op jit(solution)/shard_map/dot_general | solution.py:99
  119.1 18.7 %all-to-all-done = bf16[4,256,512]{2,1,0:T(8,128)(2,1)S(1)} async-done(((bf16[4,256,512]{2,1,0:T(8,128)(2,1)}), bf16[4,256,512]{2,1,0:T(8,128)(2,1)S(1)}, u32[]{:S(2)}, u32[]{:S(2)}) %all-to-all-start) | async-done | bytes 1048608 | tf_op jit(solution)/shard_map/all_to_all | solution.py:100
  137.8 4.4 %all-to-all-start.2 = ((bf16[4,256,1024]{2,1,0:T(8,128)(2,1)}), bf16[4,256,1024]{2,1,0:T(8,128)(2,1)}, u32[]{:S(2)}, u32[]{:S(2)}) async-start(bf16[4,256,1024]{2,1,0:T(8,128)(2,1)} %bitcast.33), calls=%async_computation.2 | async-start | bytes 4194304 | tf_op jit(solution)/shard_map/all_to_all | solution.py:100
  142.3 0.0 all-gather.5.cloned.1.call-start
  142.3 0.3 multiply_cosine_fusion
  142.6 0.8 copy.28
  143.4 0.8 copy.30
  144.2 0.7 iota_compare_fusion
  144.8 2.2 convert_reduce_fusion.1
  147.1 2.0 copy.26
  149.1 1.9 fusion.13
  151.0 1.9 copy.41
  152.9 2.0 copy.40
  154.9 0.9 reduce_sum.58
  155.8 1.8 copy.39
  157.6 2.2 subtract_convert_fusion.1
  159.8 30.2 %all-to-all-done.2 = bf16[4,256,1024]{2,1,0:T(8,128)(2,1)} async-done(((bf16[4,256,1024]{2,1,0:T(8,128)(2,1)}), bf16[4,256,1024]{2,1,0:T(8,128)(2,1)}, u32[]{:S(2)}, u32[]{:S(2)}) %all-to-all-start.2) | async-done | bytes 2097184 | tf_op jit(solution)/shard_map/all_to_all | solution.py:100
  190.1 2.1 convert_reduce_fusion
  192.2 1.3 copy.31
  193.5 1.3 subtract_convert_fusion
  194.8 0.3 copy.32
  195.1 1.0 copy.33
  196.1 3.6 %bitcast_select_fusion = f32[4,2,256,256]{2,3,1,0:T(8,128)} fusion(pred[256,256]{0,1:T(8,128)(4,1)} %iota_compare_fusion, bf16[256,4,2,64]{3,0,2,1:T(8,128)(2,1)} %bitcast.38, bf16[256,4,2,64]{3,0,2,1:T(8,128)(2,1)S(1)} %bitcast.37, bf16[256,4,64]{2,0,1:T(8,128)(2,1)} %get-tuple-element.6, bf16[256,4,64]{2,0,1:T(8,128)(2,1)} %get-tuple-element.5), kind=kOutput, calls=%fused_computation.2 | convolution fusion | flops 137363456 | bytes 2949120 | tf_op jit(solution)/shard_map/nkgd,mkd->kgnm/dot_general | solution.py:32
  199.7 3.5 %convolution_convert_fusion.4 = bf16[4,128,2,256]{3,1,2,0:T(8,128)(2,1)} fusion(bf16[256,4,128,1]{0,2,3,1:T(8,128)(2,1)S(1)} %bitcast.40, f32[4,2,256,256]{2,3,1,0:T(8,128)} %bitcast_select_fusion), kind=kOutput, calls=%fused_computation.13 | convolution fusion | flops 135530752 | bytes 2883584 | tf_op jit(solution)/shard_map/kgnm,mkd->nkgd/dot_general | solution.py:38
  203.2 0.0 all-gather.5.cloned.1.call-update
  203.2 0.0 reduce-scatter.2.cloned.1.call-start
  203.3 44.5 %all-gather.5.cloned.1.call-done = bf16[1024,1024]{0,1:T(8,128)(2,1)} async-done(((bf16[256,1024]{0,1:T(8,128)(2,1)}), bf16[1024,1024]{0,1:T(8,128)(2,1)}) %all-gather.5.cloned.1.call-update) | async-done | bytes 2097168 | tf_op jit(solution)/shard_map/all_gather | solution.py:112
  247.8 5.9 %convolution_convert_fusion = bf16[1024,1152]{1,0:T(8,128)(2,1)} fusion(bf16[1024,1024]{0,1:T(8,128)(2,1)} %all-gather.5.cloned.1.call-done, bf16[1024,1152]{1,0:T(8,128)(2,1)S(1)} %copy-done), kind=kOutput, calls=%fused_computation.1 | convolution fusion | flops 2417098752 | bytes 6815744 | tf_op jit(solution)/shard_map/dot_general | solution.py:113
  253.7 0.0 reduce-scatter.2.cloned.1.call-update
  253.7 31.1 %reduce-scatter.2.cloned.1.call-done = bf16[256,1152]{1,0:T(8,128)(2,1)} async-done(((bf16[1024,1152]{1,0:T(8,128)(2,1)}), bf16[256,1152]{1,0:T(8,128)(2,1)}) %reduce-scatter.2.cloned.1.call-update) | async-done | bytes 589840 | tf_op jit(solution)/shard_map/reduce_scatter | solution.py:114
  284.9 1.7 collective-permute-start.1
  286.6 0.2 fusion
  286.8 34.6 %psum.15 = f32[256]{0:T(256)S(1)} all-reduce(f32[256]{0:T(256)S(1)} %fusion), channel_id=1, replica_groups=mesh['groups'=2,'fsdp'=4,'tensor'=4] {'tensor'}, use_global_device_ids=true, to_apply=%region_8.9 | all-reduce | flops 256 | bytes 2048 | tf_op jit(solution)/shard_map/psum | solution.py:116
  321.3 1.3 convert_add_fusion
  (18 shorter events, 0.1 us)
Async XLA Ops:
  6.5 241.2 %copy-start = (bf16[1024,1152]{1,0:T(8,128)(2,1)S(1)}, bf16[1024,1152]{1,0:T(8,128)(2,1)}, u32[]{:S(2)}) copy-start(bf16[1024,1152]{1,0:T(8,128)(2,1)} %param.12) | copy-start | bytes 7077892
  6.5 66.3 %all-gather.3.cloned.1.call-start = ((), (), s32[]{:S(2)}) async-start(), calls=%async_computation.4 | async-start | bytes 2949120 | tf_op jit(solution)/shard_map/all_gather | solution.py:66
  18.3 0.7 collective-permute-start
  19.0 0.8 copy-start.3
  77.3 30.7 %all-to-all-start.1 = ((bf16[4,256,512]{2,1,0:T(8,128)(2,1)}), bf16[4,256,512]{2,1,0:T(8,128)(2,1)S(1)}, u32[]{:S(2)}, u32[]{:S(2)}) async-start(bf16[4,256,512]{2,1,0:T(8,128)(2,1)} %bitcast.36), calls=%async_computation.1 | async-start | bytes 2097152 | tf_op jit(solution)/shard_map/all_to_all | solution.py:100
  108.1 1.0 copy-start.2
  109.0 28.8 %all-to-all-start = ((bf16[4,256,512]{2,1,0:T(8,128)(2,1)}), bf16[4,256,512]{2,1,0:T(8,128)(2,1)S(1)}, u32[]{:S(2)}, u32[]{:S(2)}) async-start(bf16[4,256,512]{2,1,0:T(8,128)(2,1)} %bitcast.35), calls=%async_computation | async-start | bytes 2097152 | tf_op jit(solution)/shard_map/all_to_all | solution.py:100
  137.8 52.3 %all-to-all-start.2 = ((bf16[4,256,1024]{2,1,0:T(8,128)(2,1)}), bf16[4,256,1024]{2,1,0:T(8,128)(2,1)}, u32[]{:S(2)}, u32[]{:S(2)}) async-start(bf16[4,256,1024]{2,1,0:T(8,128)(2,1)} %bitcast.33), calls=%async_computation.2 | async-start | bytes 4194304 | tf_op jit(solution)/shard_map/all_to_all | solution.py:100
  142.3 105.5 %all-gather.5.cloned.1.call-start = ((), (), s32[]{:S(2)}) async-start(), calls=%async_computation.5 | async-start | bytes 2621440 | tf_op jit(solution)/shard_map/all_gather | solution.py:112
  196.1 3.6 %copy-start.4 = (bf16[256,512]{0,1:T(8,128)(2,1)S(1)}, bf16[256,512]{0,1:T(8,128)(2,1)}, u32[]{:S(2)}) copy-start(bf16[256,512]{0,1:T(8,128)(2,1)} %copy.39) | copy-start | bytes 786436
  203.2 81.7 %reduce-scatter.2.cloned.1.call-start = ((), (), s32[]{:S(2)}) async-start(), calls=%async_computation.6 | async-start | bytes 2949120 | tf_op jit(solution)/shard_map/reduce_scatter | solution.py:114
  253.7 32.9 %copy-start.5 = (bf16[1152]{0:T(1024)(128)(2,1)S(1)}, bf16[1152]{0:T(1024)(128)(2,1)}, u32[]{:S(2)}) copy-start(bf16[1152]{0:T(1024)(128)(2,1)} %param.13) | copy-start | bytes 6916
  253.7 67.7 %copy-start.1 = (bf16[256,1152]{1,0:T(8,128)(2,1)S(1)}, bf16[256,1152]{1,0:T(8,128)(2,1)}, u32[]{:S(2)}) copy-start(bf16[256,1152]{1,0:T(8,128)(2,1)} %param.7) | copy-start | bytes 1769476
  284.9 1.7 collective-permute-start.1
Sparse Core Ops, SparseCore 0:
  20.0 52.8 all-gather.2
  203.3 44.3 all-gather.4
  253.8 30.9 reduce-scatter.1
where the time goes:
time: 330 us; the launch traced here: 329 us
  waiting for transfers between devices  199 us (60%)
  blocking collectives  42.9 us (13%)
  matrix products  28.5 us (9%)
  local copies, waits for them, and re-layouts  15.6 us (5%)
  starting transfers between devices  15 us (5%)
  other arithmetic  14.6 us (4%)
  between operations  13.2 us (4%)
    all_to_all x3, waiting for transfers between devices, on_device(): parts = lax.all_to_all(part, 'fsdp', 0, 0, tiled=True)  70.5 us
    all_gather x1, waiting for transfers between devices, to_rows(): return lax.all_gather(held, 'tensor', axis=0, tiled=True)  53 us
    all_gather x1, waiting for transfers between devices, on_device(): attn_all = lax.all_gather(attn, 'fsdp', axis=0, tiled=True)  44.5 us
    psum x1, blocking collectives, on_device(): post_total = lax.psum(jnp.sum(proj * proj, axis=1), 'tensor')  34.6 us
    reduce_scatter x1, waiting for transfers between devices, on_device(): summed = lax.psum_scatter(part, 'tensor', scatter_dimension=0, tiled=True)  31.1 us
    dot_general x3, matrix products, on_device(): jnp.dot(mine, piece, preferred_element_type=jnp.float32)  15.5 us
    all_to_all x3, starting transfers between devices, on_device(): parts = lax.all_to_all(part, 'fsdp', 0, 0, tiled=True)  12.6 us
    psum x1, blocking collectives, on_device(): total = lax.psum(jnp.sum(widened * widened, axis=1), 'tensor')  8.37 us
  transfers between devices with their start and end apart: 8, of which 6 were waited for; matrix products, arithmetic and copies ran while one was open for 9% of the time, Pallas kernels for 0%

commit v1 on v0

--- a/solution.py
+++ b/solution.py
@@ -8,6 +8,11 @@
 soft_cap = 50.0
 attn_scale = 144.0 ** (-0.5)
 rope_base = 10000.0
+
+
+def exchange_gather(array, name, along):
+    sent = jnp.stack([array] * lax.axis_size(name))
+    return jnp.concatenate(lax.all_to_all(sent, name, 0, 0), axis=along)
 
 
 def rotate(values, position):
@@ -63,7 +68,7 @@
             got = lax.ppermute(piece, ("fsdp", "tensor"), swap_pairs(n_fsdp, n_tensor, turn))
             held = lax.dynamic_update_index_in_dim(held, got, (f - turn) % ratio, 0)
         held = held.reshape(ratio * rows, width)
-    return lax.all_gather(held, "tensor", axis=0, tiled=True)
+    return exchange_gather(held, "tensor", 0)
 
 
 def from_rows(summed, rows, n_fsdp, n_tensor):

time: 330 us -> 335 us (1.015)
  blocking collectives: 42.9 us -> 104 us
  waiting for transfers between devices: 199 us -> 146 us
    all_to_all x0 -> x1, blocking collectives: none -> 61.5 us  [exchange_gather(): return jnp.concatenate(lax.all_to_all(sent, name, 0, 0), axis=along)]
    all_gather x1 -> x0, waiting for transfers between devices: 53 us -> none  [to_rows(): return lax.all_gather(held, 'tensor', axis=0, tiled=True)]
  transfers between devices with their start and end apart: 8 -> 7, of which waited for: 6 -> 5; matrix products, arithmetic and copies ran while one was open for 9% -> 9% of each run, Pallas kernels for 0% -> 0%
where the time goes in v1:
time: 335 us; the launch traced here: 334 us
  waiting for transfers between devices  146 us (44%)
  blocking collectives  104 us (31%)
  matrix products  26.5 us (8%)
  local copies, waits for them, and re-layouts  14.9 us (4%)
  other arithmetic  14.6 us (4%)
  starting transfers between devices  14 us (4%)
  between operations  13.5 us (4%)
    all_to_all x3, waiting for transfers between devices, on_device(): parts = lax.all_to_all(part, 'fsdp', 0, 0, tiled=True)  70.1 us
    all_to_all x1, blocking collectives, exchange_gather(): return jnp.concatenate(lax.all_to_all(sent, name, 0, 0), axis=along)  61.5 us
    all_gather x1, waiting for transfers between devices, on_device(): attn_all = lax.all_gather(attn, 'fsdp', axis=0, tiled=True)  44.8 us
    psum x1, blocking collectives, on_device(): post_total = lax.psum(jnp.sum(proj * proj, axis=1), 'tensor')  34.6 us
    reduce_scatter x1, waiting for transfers between devices, on_device(): summed = lax.psum_scatter(part, 'tensor', scatter_dimension=0, tiled=True)  31.1 us
    dot_general x3, matrix products, on_device(): jnp.dot(mine, piece, preferred_element_type=jnp.float32)  13.5 us
    all_to_all x3, starting transfers between devices, on_device(): parts = lax.all_to_all(part, 'fsdp', 0, 0, tiled=True)  11.5 us
    psum x1, blocking collectives, on_device(): total = lax.psum(jnp.sum(widened * widened, axis=1), 'tensor')  8.37 us
  transfers between devices with their start and end apart: 7, of which 5 were waited for; matrix products, arithmetic and copies ran while one was open for 9% of the time, Pallas kernels for 0%

profile of v1, /device:TPU:0, one launch (start us, length us, event | category | flops | bytes accessed | tf_op | source)
XLA Modules:
  0.0 334.1 jit_solution(2577082363246909949)
XLA Ops:
  6.5 1.4 fusion.2
  7.9 8.4 %psum.14 = f32[256]{0:T(256)S(1)} all-reduce(f32[256]{0:T(256)S(1)} %fusion.2), channel_id=1, replica_groups=mesh['groups'=2,'fsdp'=4,'tensor'=4] {'tensor'}, use_global_device_ids=true, to_apply=%region_1.0 | all-reduce | flops 256 | bytes 2048 | tf_op jit(solution)/shard_map/psum | solution.py:97
  16.3 0.7 convert_element_type.74
  17.0 1.3 fusion.4
  18.3 0.7 collective-permute-start
  19.0 0.2 stack.2
  19.2 0.0 copy-start.6
  19.2 61.5 %all_to_all.32 = bf16[4,256,1152]{2,1,0:T(8,128)(2,1)S(1)} all-to-all(bf16[4,256,1152]{2,1,0:T(8,128)(2,1)S(1)} %stack.2), channel_id=1, replica_groups=mesh['groups'=2,'fsdp'=4,'tensor'=4] {'tensor'}, dimensions={0} | all-to-all | bytes 4718592 | tf_op jit(solution)/shard_map/all_to_all | solution.py:15
  80.7 2.5 convolution_convert_fusion.2
  83.2 3.5 %all-to-all-start.2 = ((bf16[4,256,512]{2,1,0:T(8,128)(2,1)}), bf16[4,256,512]{2,1,0:T(8,128)(2,1)S(1)}, u32[]{:S(2)}, u32[]{:S(2)}) async-start(bf16[4,256,512]{2,1,0:T(8,128)(2,1)} %bitcast.40), calls=%async_computation.2 | async-start | bytes 2097152 | tf_op jit(solution)/shard_map/all_to_all | solution.py:105
  86.7 4.5 %convolution_convert_fusion.3 = bf16[1024,512]{1,0:T(8,128)(2,1)} fusion(bf16[1024,1152]{1,0:T(8,128)(2,1)} %bitcast.35, bf16[1152,512]{1,0:T(8,128)(2,1)} %param.11), kind=kOutput, calls=%fused_computation.10 | convolution fusion | flops 1208483840 | bytes 4587520 | tf_op jit(solution)/shard_map/dot_general | solution.py:104
  91.2 21.1 %all-to-all-done.2 = bf16[4,256,512]{2,1,0:T(8,128)(2,1)S(1)} async-done(((bf16[4,256,512]{2,1,0:T(8,128)(2,1)}), bf16[4,256,512]{2,1,0:T(8,128)(2,1)S(1)}, u32[]{:S(2)}, u32[]{:S(2)}) %all-to-all-start.2) | async-done | bytes 1048608 | tf_op jit(solution)/shard_map/all_to_all | solution.py:105
  112.3 1.0 copy-done.2
  113.3 3.5 %all-to-all-start.1 = ((bf16[4,256,512]{2,1,0:T(8,128)(2,1)}), bf16[4,256,512]{2,1,0:T(8,128)(2,1)S(1)}, u32[]{:S(2)}, u32[]{:S(2)}) async-start(bf16[4,256,512]{2,1,0:T(8,128)(2,1)} %bitcast.39), calls=%async_computation.1 | async-start | bytes 2097152 | tf_op jit(solution)/shard_map/all_to_all | solution.py:105
  116.8 6.6 %convolution_convert_fusion.1 = bf16[1024,1024]{1,0:T(8,128)(2,1)} fusion(bf16[1024,1152]{1,0:T(8,128)(2,1)} %bitcast.36, bf16[1152,1024]{1,0:T(8,128)(2,1)} %param.9), kind=kOutput, calls=%fused_computation.5 | convolution fusion | flops 2416967680 | bytes 6815744 | tf_op jit(solution)/shard_map/dot_general | solution.py:104
  123.4 18.7 %all-to-all-done.1 = bf16[4,256,512]{2,1,0:T(8,128)(2,1)S(1)} async-done(((bf16[4,256,512]{2,1,0:T(8,128)(2,1)}), bf16[4,256,512]{2,1,0:T(8,128)(2,1)S(1)}, u32[]{:S(2)}, u32[]{:S(2)}) %all-to-all-start.1) | async-done | bytes 1048608 | tf_op jit(solution)/shard_map/all_to_all | solution.py:105
  142.1 4.4 %all-to-all-start.3 = ((bf16[4,256,1024]{2,1,0:T(8,128)(2,1)}), bf16[4,256,1024]{2,1,0:T(8,128)(2,1)}, u32[]{:S(2)}, u32[]{:S(2)}) async-start(bf16[4,256,1024]{2,1,0:T(8,128)(2,1)} %bitcast.37), calls=%async_computation.3 | async-start | bytes 4194304 | tf_op jit(solution)/shard_map/all_to_all | solution.py:105
  146.5 0.0 all-gather.2.cloned.1.call-start
  146.6 0.3 multiply_cosine_fusion
  146.9 0.8 copy.28
  147.7 0.8 copy.30
  148.4 0.6 iota_compare_fusion
  149.1 2.2 convert_reduce_fusion.1
  151.3 2.0 copy.26
  153.3 1.9 fusion.13
  155.2 1.9 copy.41
  157.2 1.9 copy.40
  159.1 0.9 reduce_sum.58
  160.0 1.8 copy.39
  161.9 2.2 subtract_convert_fusion.1
  164.1 30.3 %all-to-all-done.3 = bf16[4,256,1024]{2,1,0:T(8,128)(2,1)} async-done(((bf16[4,256,1024]{2,1,0:T(8,128)(2,1)}), bf16[4,256,1024]{2,1,0:T(8,128)(2,1)}, u32[]{:S(2)}, u32[]{:S(2)}) %all-to-all-start.3) | async-done | bytes 2097184 | tf_op jit(solution)/shard_map/all_to_all | solution.py:105
  194.3 2.1 convert_reduce_fusion
  196.4 1.3 copy.31
  197.7 1.3 subtract_convert_fusion
  199.1 0.3 copy.32
  199.4 1.0 copy.33
  200.4 3.6 %bitcast_select_fusion = f32[4,2,256,256]{2,3,1,0:T(8,128)} fusion(pred[256,256]{0,1:T(8,128)(4,1)} %iota_compare_fusion, bf16[256,4,2,64]{3,0,2,1:T(8,128)(2,1)} %bitcast.42, bf16[256,4,2,64]{3,0,2,1:T(8,128)(2,1)S(1)} %bitcast.41, bf16[256,4,64]{2,0,1:T(8,128)(2,1)} %get-tuple-element.6, bf16[256,4,64]{2,0,1:T(8,128)(2,1)} %get-tuple-element.5), kind=kOutput, calls=%fused_computation.2 | convolution fusion | flops 137363456 | bytes 2949120 | tf_op jit(solution)/shard_map/nkgd,mkd->kgnm/dot_general | solution.py:37
  204.0 3.5 %convolution_convert_fusion.4 = bf16[4,128,2,256]{3,1,2,0:T(8,128)(2,1)} fusion(bf16[256,4,128,1]{0,2,3,1:T(8,128)(2,1)S(1)} %bitcast.44, f32[4,2,256,256]{2,3,1,0:T(8,128)} %bitcast_select_fusion), kind=kOutput, calls=%fused_computation.13 | convolution fusion | flops 135530752 | bytes 2883584 | tf_op jit(solution)/shard_map/kgnm,mkd->nkgd/dot_general | solution.py:43
  207.5 0.0 all-gather.2.cloned.1.call-update
  207.5 0.0 reduce-scatter.2.cloned.1.call-start
  207.5 44.8 %all-gather.2.cloned.1.call-done = bf16[1024,1024]{0,1:T(8,128)(2,1)} async-done(((bf16[256,1024]{0,1:T(8,128)(2,1)}), bf16[1024,1024]{0,1:T(8,128)(2,1)}) %all-gather.2.cloned.1.call-update) | async-done | bytes 2097168 | tf_op jit(solution)/shard_map/all_gather | solution.py:117
  252.4 5.9 %convolution_convert_fusion = bf16[1024,1152]{1,0:T(8,128)(2,1)} fusion(bf16[1024,1024]{0,1:T(8,128)(2,1)} %all-gather.2.cloned.1.call-done, bf16[1024,1152]{1,0:T(8,128)(2,1)S(1)} %copy-done), kind=kOutput, calls=%fused_computation.1 | convolution fusion | flops 2417098752 | bytes 6815744 | tf_op jit(solution)/shard_map/dot_general | solution.py:118
  258.3 0.0 reduce-scatter.2.cloned.1.call-update
  258.3 31.1 %reduce-scatter.2.cloned.1.call-done = bf16[256,1152]{1,0:T(8,128)(2,1)} async-done(((bf16[1024,1152]{1,0:T(8,128)(2,1)}), bf16[256,1152]{1,0:T(8,128)(2,1)}) %reduce-scatter.2.cloned.1.call-update) | async-done | bytes 589840 | tf_op jit(solution)/shard_map/reduce_scatter | solution.py:119
  289.5 1.7 collective-permute-start.1
  291.2 0.2 fusion
  291.4 34.6 %psum.15 = f32[256]{0:T(256)S(1)} all-reduce(f32[256]{0:T(256)S(1)} %fusion), channel_id=1, replica_groups=mesh['groups'=2,'fsdp'=4,'tensor'=4] {'tensor'}, use_global_device_ids=true, to_apply=%region_8.9 | all-reduce | flops 256 | bytes 2048 | tf_op jit(solution)/shard_map/psum | solution.py:121
  326.0 1.3 convert_add_fusion
  (19 shorter events, 0.1 us)
Async XLA Ops:
  6.5 245.8 %copy-start = (bf16[1024,1152]{1,0:T(8,128)(2,1)S(1)}, bf16[1024,1152]{1,0:T(8,128)(2,1)}, u32[]{:S(2)}) copy-start(bf16[1024,1152]{1,0:T(8,128)(2,1)} %param.12) | copy-start | bytes 7077892
  18.3 0.7 collective-permute-start
  19.2 61.5 %copy-start.6 = (bf16[1152,512]{1,0:T(8,128)(2,1)S(1)}, bf16[1152,512]{1,0:T(8,128)(2,1)}, u32[]{:S(2)}) copy-start(bf16[1152,512]{1,0:T(8,128)(2,1)} %param.10) | copy-start | bytes 3538948
  80.7 2.5 copy-start.3
  83.2 29.1 %all-to-all-start.2 = ((bf16[4,256,512]{2,1,0:T(8,128)(2,1)}), bf16[4,256,512]{2,1,0:T(8,128)(2,1)S(1)}, u32[]{:S(2)}, u32[]{:S(2)}) async-start(bf16[4,256,512]{2,1,0:T(8,128)(2,1)} %bitcast.40), calls=%async_computation.2 | async-start | bytes 2097152 | tf_op jit(solution)/shard_map/all_to_all | solution.py:105
  112.3 1.0 copy-start.2
  113.3 28.8 %all-to-all-start.1 = ((bf16[4,256,512]{2,1,0:T(8,128)(2,1)}), bf16[4,256,512]{2,1,0:T(8,128)(2,1)S(1)}, u32[]{:S(2)}, u32[]{:S(2)}) async-start(bf16[4,256,512]{2,1,0:T(8,128)(2,1)} %bitcast.39), calls=%async_computation.1 | async-start | bytes 2097152 | tf_op jit(solution)/shard_map/all_to_all | solution.py:105
  142.1 52.3 %all-to-all-start.3 = ((bf16[4,256,1024]{2,1,0:T(8,128)(2,1)}), bf16[4,256,1024]{2,1,0:T(8,128)(2,1)}, u32[]{:S(2)}, u32[]{:S(2)}) async-start(bf16[4,256,1024]{2,1,0:T(8,128)(2,1)} %bitcast.37), calls=%async_computation.3 | async-start | bytes 4194304 | tf_op jit(solution)/shard_map/all_to_all | solution.py:105
  146.5 105.8 %all-gather.2.cloned.1.call-start = ((), (), s32[]{:S(2)}) async-start(), calls=%async_computation.5 | async-start | bytes 2621440 | tf_op jit(solution)/shard_map/all_gather | solution.py:117
  200.4 3.6 %copy-start.4 = (bf16[256,512]{0,1:T(8,128)(2,1)S(1)}, bf16[256,512]{0,1:T(8,128)(2,1)}, u32[]{:S(2)}) copy-start(bf16[256,512]{0,1:T(8,128)(2,1)} %copy.39) | copy-start | bytes 786436
  207.5 82.0 %reduce-scatter.2.cloned.1.call-start = ((), (), s32[]{:S(2)}) async-start(), calls=%async_computation.6 | async-start | bytes 2949120 | tf_op jit(solution)/shard_map/reduce_scatter | solution.py:119
  258.3 32.9 %copy-start.5 = (bf16[1152]{0:T(1024)(128)(2,1)S(1)}, bf16[1152]{0:T(1024)(128)(2,1)}, u32[]{:S(2)}) copy-start(bf16[1152]{0:T(1024)(128)(2,1)} %param.13) | copy-start | bytes 6916
  258.3 67.7 %copy-start.1 = (bf16[256,1152]{1,0:T(8,128)(2,1)S(1)}, bf16[256,1152]{1,0:T(8,128)(2,1)}, u32[]{:S(2)}) copy-start(bf16[256,1152]{1,0:T(8,128)(2,1)} %param.7) | copy-start | bytes 1769476
  289.5 1.7 collective-permute-start.1
Sparse Core Ops, SparseCore 0:
  207.6 44.7 all-gather.1
  258.4 30.9 reduce-scatter.1
